TPU v7x, 32 devices: a whole 2x2x4 slice. The times are simulated.
32 devices in a mesh: unit: 4 (over y, x), replica: 2 (over core), model: 4 (over z).
Axes of the slice: x: 2, y: 2, z: 4, core: 2. Of those that a mesh axis runs over, the one named last changes fastest.
Arguments:
- slope_up: float32 [8, 768, 3072], P(('unit', 'replica'), None, 'model'), parts along dimension 0, may hold values from -0.875 to 0.875
- slope_down: float32 [8, 3072, 768], P(('unit', 'replica'), 'model'), parts along dimension 0, may hold values from -0.875 to 0.875
- slope_query: float32 [8, 768, 768], P(('unit', 'replica'), None, 'model'), parts along dimension 0, may hold values from -0.875 to 0.875
- slope_key: float32 [8, 768, 768], P(('unit', 'replica'), None, 'model'), parts along dimension 0, may hold values from -0.875 to 0.875
- slope_value: float32 [8, 768, 768], P(('unit', 'replica'), None, 'model'), parts along dimension 0, may hold values from -0.875 to 0.875
- slope_mixed: float32 [8, 768, 768], P(('unit', 'replica'), 'model'), parts along dimension 0, may hold values from -0.875 to 0.875
- slope_norm: float32 [8, 768], P(('unit', 'replica')), parts along dimension 0, may hold values from -8 to 8
- param_up: float32 [3072, 3072], P(('unit', 'replica'), 'model'), parts along dimension 0, may hold values from -0.21875 to 0.21875
- param_down: float32 [12288, 768], P(('unit', 'model'), 'replica'), parts along dimension 0, may hold values from -0.109375 to 0.109375
- param_query: float32 [3072, 768], P(('unit', 'replica'), 'model'), parts along dimension 0, may hold values from -0.21875 to 0.21875
- param_key: float32 [3072, 768], P(('unit', 'replica'), 'model'), parts along dimension 0, may hold values from -0.21875 to 0.21875
- param_value: float32 [3072, 768], P(('unit', 'replica'), 'model'), parts along dimension 0, may hold values from -0.21875 to 0.21875
- param_mixed: float32 [3072, 768], P(('unit', 'model'), 'replica'), parts along dimension 0, may hold values from -0.21875 to 0.21875
- param_norm: float32 [3072], P(('unit', 'replica')), parts along dimension 0, may hold values from 0.25 to 1.75
Outputs:
- half_up: bfloat16 [3072, 3072], P('unit', 'model'), parts along dimension 0
- half_down: bfloat16 [12288, 768], P(('unit', 'model')), parts along dimension 0
- half_query: bfloat16 [3072, 768], P('unit', 'model'), parts along dimension 0
- half_key: bfloat16 [3072, 768], P('unit', 'model'), parts along dimension 0
- half_value: bfloat16 [3072, 768], P('unit', 'model'), parts along dimension 0
- half_mixed: bfloat16 [3072, 768], P(('unit', 'model')), parts along dimension 0
- half_norm: bfloat16 [3072], P('unit'), parts along dimension 0
- next_up: float32 [3072, 3072], P(('unit', 'replica'), 'model'), parts along dimension 0
- next_down: float32 [12288, 768], P(('unit', 'model'), 'replica'), parts along dimension 0
- next_query: float32 [3072, 768], P(('unit', 'replica'), 'model'), parts along dimension 0
- next_key: float32 [3072, 768], P(('unit', 'replica'), 'model'), parts along dimension 0
- next_value: float32 [3072, 768], P(('unit', 'replica'), 'model'), parts along dimension 0
- next_mixed: float32 [3072, 768], P(('unit', 'model'), 'replica'), parts along dimension 0
- next_norm: float32 [3072], P(('unit', 'replica')), parts along dimension 0
There are 4 independent parts, one for each index of `unit`. A program takes and returns all parts, laid end to end along the dimension named above; each array names one. Nothing has to cross between parts.
All inputs are finite; a program needn't handle non-finite values.
Results may differ from a plain program's by a relative error of at most 0.001.
Values may be sent and summed in bfloat16 or wider, within the bound.
A program may use at most 64 MiB of HBM per device.

v0:
```python
import functools

import jax
import jax.numpy as jnp
from jax import lax
from jax.experimental import pallas as pl
from jax.experimental.pallas import tpu as pltpu
from jax.sharding import PartitionSpec as P

learn_rate = 0.3
ANY = pl.BlockSpec(memory_space=pl.ANY)
VMEM_BYTES = 67043328


def pieces(shape, split_rows, parts):
    rows = shape[0]
    if rows % (16 * parts):
        parts = 1
    return [(part * (rows // parts), rows // parts) for part in range(parts)]


def plan(halves, by_row, small):
    chunks = []
    for at, half in enumerate(halves):
        parts = max(1, half[0] * half[1] // small)
        chunks += [(at, start, rows) for start, rows in pieces(half, by_row[at], parts)]
    return chunks


def exchange(n, by_row, chunks, rate, *refs):
    m = len(by_row)
    slopes, slope_norm = refs[:m], refs[m]
    params, param_norm = refs[m + 1 : 2 * m + 1], refs[2 * m + 1]
    refs = refs[2 * m + 2 :]
    halfs, norm_half = refs[:m], refs[m]
    kept, norm_next = refs[m + 1 : 2 * m + 1], refs[2 * m + 1]
    refs = refs[2 * m + 2 :]
    own, got = refs[:m], refs[m : 2 * m]
    (norms, norm_own, norm_got, norm_all, in_sem, keep_sem, send_sem, recv_sem,
     back_send, back_recv, norm_in, norm_send, norm_recv) = refs[2 * m :]

    me = lax.axis_index("replica")
    peer = 1 - me
    there = {"replica": peer}

    def half_of(at, who, start, rows):
        height, width = kept[at].shape
        if by_row[at]:
            return pl.ds(pl.multiple_of(who * height + start, 16), rows), pl.ds(0, width)
        return pl.ds(start, rows), pl.ds(pl.multiple_of(who * width, width), width)

    def remote(source, target, out_sem, in_sem):
        return pltpu.make_async_remote_copy(
            src_ref=source,
            dst_ref=target,
            send_sem=out_sem,
            recv_sem=in_sem,
            device_id=there,
            device_id_type=pl.DeviceIdType.MESH,
        )

    loads = []
    for c, (at, start, rows) in enumerate(chunks):
        mine = pl.ds(start, rows)
        loads.append((
            pltpu.make_async_copy(
                slopes[at].at[(0, *half_of(at, me, start, rows))], own[at].at[mine], in_sem.at[c]
            ),
            pltpu.make_async_copy(params[at].at[mine], kept[at].at[mine], keep_sem.at[c]),
        ))
    norm_loads = (
        pltpu.make_async_copy(slope_norm, norms.at[pl.ds(me, 1)], norm_in.at[0]),
        pltpu.make_async_copy(param_norm, norm_own, norm_in.at[1]),
    )

    barrier = pltpu.get_barrier_semaphore()
    pl.semaphore_signal(barrier, inc=1, device_id=there, device_id_type=pl.DeviceIdType.MESH)
    pl.semaphore_wait(barrier, 1)

    norm_sends = [
        remote(slope_norm, norms.at[pl.ds(me, 1)], norm_send.at[0], norm_recv.at[0]),
        remote(param_norm, norm_got, norm_send.at[1], norm_recv.at[1]),
    ]
    sends = [
        remote(
            slopes[at].at[(0, *half_of(at, peer, start, rows))],
            got[at].at[pl.ds(start, rows)],
            send_sem.at[c],
            recv_sem.at[c],
        )
        for c, (at, start, rows) in enumerate(chunks)
    ]
    for send in sends + norm_sends:
        send.start()
    for load in loads:
        load[0].start()
        load[1].start()
    for load in norm_loads:
        load.start()

    backs = []
    for c, (at, start, rows) in enumerate(chunks):
        loads[c][0].wait()
        loads[c][1].wait()
        sends[c].wait_recv()
        step = 32 if rows % 32 == 0 else 16
        height, width = kept[at].shape

        @pl.loop(0, rows // step)
        def update(block, at=at, start=start, step=step, height=height, width=width):
            first = pl.multiple_of(start + block * step, step)
            span = pl.ds(first, step)
            mean = (own[at][span] + got[at][span]) * rate
            moved = kept[at][span] - learn_rate * mean
            kept[at][span] = moved
            halfs[at][half_of(at, me, first, step)] = moved.astype(jnp.bfloat16)

        place = half_of(at, me, start, rows)
        back = remote(halfs[at].at[place], halfs[at].at[place], back_send.at[c], back_recv.at[c])
        back.start()
        backs.append(back)

    for load in norm_loads:
        load.wait()
    for send in norm_sends:
        send.wait_recv()
    width = norm_own.shape[0]
    total = norms[0:1] + norms[1:2]
    for where, held in ((me, norm_own), (peer, norm_got)):
        cut = pl.ds(pl.multiple_of(where * width, width), width)
        norm_all[0:1, cut] = held[...].reshape(1, width)
    moved = norm_all[...] - learn_rate * (total * rate)
    norm_all[...] = moved
    norm_half[...] = moved.reshape(n * width).astype(jnp.bfloat16)
    cut = pl.ds(pl.multiple_of(me * width, width), width)
    norm_next[...] = norm_all[0:1, cut].reshape(width)

    for send in sends + norm_sends:
        send.wait_send()
    for back in backs:
        back.wait()


def settle(count, *refs):
    sems = refs[-1]
    copies = [
        pltpu.make_async_copy(refs[k], refs[count + k], sems.at[k]) for k in range(count)
    ]
    for copy in copies:
        copy.start()
    for copy in copies:
        copy.wait()


def shards(n, *arrays):
    m = len(arrays) // 2 - 1
    slopes, slope_norm = list(arrays[:m]), arrays[m]
    params, param_norm = list(arrays[m + 1 : -1]), arrays[-1]
    turned = [2, 3, 4]
    by_row = [slope.shape[1] != param.shape[0] for slope, param in zip(slopes, params)]
    for at in turned:
        slopes[at] = slopes[at].transpose(0, 2, 1)
        params[at] = params[at].T
        by_row[at] = not by_row[at]
    f32, bf16 = jnp.float32, jnp.bfloat16
    halves = [param.shape for param in params]
    wholes = [slope.shape[1:] for slope in slopes]
    small = min(half[0] * half[1] for half in halves)
    chunks = plan(halves, by_row, 4 * small)
    count = len(chunks)
    width = param_norm.shape[0]
    dma = pltpu.SemaphoreType.DMA
    results = sum(rows * columns for rows, columns in wholes) * 2
    results += sum(rows * columns for rows, columns in halves) * 4
    outs = pl.pallas_call(
        functools.partial(exchange, n, by_row, chunks, n ** (-0.5)),
        out_shape=(
            *[pltpu.VMEM(whole, bf16) for whole in wholes],
            pltpu.VMEM((n * width,), bf16),
            *[pltpu.VMEM(half, f32) for half in halves],
            pltpu.VMEM((width,), f32),
        ),
        in_specs=[ANY] * (2 * m + 2),
        out_specs=[pl.BlockSpec(memory_space=pltpu.VMEM)] * (2 * m + 2),
        scratch_shapes=[
            *[pltpu.VMEM(half, f32) for half in halves * 2],
            pltpu.VMEM((n, n * width), f32),
            pltpu.VMEM((width,), f32),
            pltpu.VMEM((width,), f32),
            pltpu.VMEM((1, n * width), f32),
            *[dma((count,))] * 6,
            *[dma((2,))] * 3,
        ],
        compiler_params=pltpu.CompilerParams(
            collective_id=0, has_side_effects=True, vmem_limit_bytes=VMEM_BYTES - results - 192 * 1024
        ),
        name="exchange",
    )(*slopes, slope_norm, *params, param_norm)
    outs = list(pl.pallas_call(
        functools.partial(settle, len(outs)),
        out_shape=[jax.ShapeDtypeStruct(out.shape, out.dtype) for out in outs],
        in_specs=[pl.BlockSpec(memory_space=pltpu.VMEM)] * len(outs),
        out_specs=[ANY] * len(outs),
        scratch_shapes=[dma((len(outs),))],
        compiler_params=pltpu.CompilerParams(vmem_limit_bytes=2 * 1024 * 1024),
        name="settle",
    )(*outs))
    for at in turned:
        outs[at] = outs[at].T
        outs[m + 1 + at] = outs[m + 1 + at].T
    return tuple(outs)


def spread(
    slope_up,
    slope_down,
    slope_query,
    slope_key,
    slope_value,
    slope_mixed,
    slope_norm,
    param_up,
    param_down,
    param_query,
    param_key,
    param_value,
    param_mixed,
    param_norm,
):
    mean_up, mean_down, mean_query, mean_key, mean_value, mean_mixed = (
        lax.psum_scatter(slope_up[0], "replica", scatter_dimension=0, tiled=True),
        lax.psum_scatter(slope_down[0], "replica", scatter_dimension=1, tiled=True),
        lax.psum_scatter(slope_query[0], "replica", scatter_dimension=0, tiled=True),
        lax.psum_scatter(slope_key[0], "replica", scatter_dimension=0, tiled=True),
        lax.psum_scatter(slope_value[0], "replica", scatter_dimension=0, tiled=True),
        lax.psum_scatter(slope_mixed[0], "replica", scatter_dimension=1, tiled=True),
    )
    whole_norm = lax.psum(slope_norm[0], "replica")
    place = lax.axis_index("replica")
    mean_norm = lax.dynamic_slice_in_dim(
        whole_norm, place * param_norm.shape[0], param_norm.shape[0]
    )
    mean_rate = lax.axis_size("replica") ** (-0.5)
    mean_up = mean_up * mean_rate
    mean_down = mean_down * mean_rate
    mean_query = mean_query * mean_rate
    mean_key = mean_key * mean_rate
    mean_value = mean_value * mean_rate
    mean_mixed = mean_mixed * mean_rate
    mean_norm = mean_norm * mean_rate
    next_up = param_up - learn_rate * mean_up
    next_down = param_down - learn_rate * mean_down
    next_query = param_query - learn_rate * mean_query
    next_key = param_key - learn_rate * mean_key
    next_value = param_value - learn_rate * mean_value
    next_mixed = param_mixed - learn_rate * mean_mixed
    next_norm = param_norm - learn_rate * mean_norm
    half_up, half_down, half_query, half_key, half_value, half_mixed, half_norm = (
        lax.all_gather(next_up.astype(jnp.bfloat16), "replica", axis=0, tiled=True),
        lax.all_gather(next_down.astype(jnp.bfloat16), "replica", axis=1, tiled=True),
        lax.all_gather(next_query.astype(jnp.bfloat16), "replica", axis=0, tiled=True),
        lax.all_gather(next_key.astype(jnp.bfloat16), "replica", axis=0, tiled=True),
        lax.all_gather(next_value.astype(jnp.bfloat16), "replica", axis=0, tiled=True),
        lax.all_gather(next_mixed.astype(jnp.bfloat16), "replica", axis=1, tiled=True),
        lax.all_gather(next_norm.astype(jnp.bfloat16), "replica", axis=0, tiled=True),
    )
    return (
        half_up,
        half_down,
        half_query,
        half_key,
        half_value,
        half_mixed,
        half_norm,
        next_up,
        next_down,
        next_query,
        next_key,
        next_value,
        next_mixed,
        next_norm,
    )


def solution(mesh):
    placed = (
        P(("unit", "replica"), None, "model"),
        P(("unit", "replica"), "model", None),
        P(("unit", "replica"), None, "model"),
        P(("unit", "replica"), None, "model"),
        P(("unit", "replica"), None, "model"),
        P(("unit", "replica"), "model", None),
        P(("unit", "replica"), None),
        P(("unit", "replica"), "model"),
        P(("unit", "model"), "replica"),
        P(("unit", "replica"), "model"),
        P(("unit", "replica"), "model"),
        P(("unit", "replica"), "model"),
        P(("unit", "model"), "replica"),
        P(("unit", "replica")),
    )
    n = mesh.shape["replica"]
    return jax.shard_map(
        functools.partial(shards, n) if n == 2 else spread,
        mesh=mesh,
        in_specs=placed,
        out_specs=(
            P("unit", "model"),
            P(("unit", "model"), None),
            P("unit", "model"),
            P("unit", "model"),
            P("unit", "model"),
            P(("unit", "model"), None),
            P("unit"),
            P(("unit", "replica"), "model"),
            P(("unit", "model"), "replica"),
            P(("unit", "replica"), "model"),
            P(("unit", "replica"), "model"),
            P(("unit", "replica"), "model"),
            P(("unit", "model"), "replica"),
            P(("unit", "replica")),
        ),
        check_vma=False,
    )
```

profile of v0, /device:TPU:3, one launch (start us, length us, event | category | flops | bytes accessed | tf_op | source)
XLA Modules:
  0.0 13.4 jit_solution(7361197397528209399)
XLA Ops:
  0.7 9.7 %exchange.1 = (bf16[768,768]{1,0:T(8,128)(2,1)S(1)}, bf16[768,768]{1,0:T(8,128)(2,1)S(1)}, bf16[192,768]{1,0:T(8,128)(2,1)S(1)}, bf16[192,768]{1,0:T(8,128)(2,1)...) custom-call(f32[1,768,768]{2,1,0:T(8,128)} %refs_0_.1, ...), custom_call_target="tpu_custom_call" | custom-call | tf_op jit(solution)/shard_map/exchange/pallas_call | solution.py:175
  10.4 3.0 %settle.1 = (bf16[768,768]{1,0:T(8,128)(2,1)}, bf16[768,768]{1,0:T(8,128)(2,1)}, bf16[192,768]{1,0:T(8,128)(2,1)}, bf16[192,768]{1,0:T(8,128)(2,1)}, bf16[192,76...) custom-call(bf16[768,768]{1,0:T(8,128)(2,1)S(1)} %get-tuple-element., ...), custom_call_target="tpu_custom_call" | custom-call | tf_op jit(solution)/shard_map/settle/pallas_call | solution.py:199
where the time goes:
time: 13.6 us; the launch traced here: 13.4 us
  Pallas kernels  12.7 us (93%)
  between operations  0.66 us (5%)
    pallas_call x1, Pallas kernels, shards(): pl.pallas_call(functools.partial(exchange, n, by_row, chunks, n ** (-0.5)...  9.7 us
    pallas_call x1, Pallas kernels, shards(): pl.pallas_call(functools.partial(settle, len(outs)), out_shape=[jax.Shape...  3.03 us

commit v1 on v0

--- a/solution.py
+++ b/solution.py
@@ -8,26 +8,45 @@
 from jax.sharding import PartitionSpec as P
 
 learn_rate = 0.3
+LOG2E = 1.4426950408889634
 ANY = pl.BlockSpec(memory_space=pl.ANY)
 VMEM_BYTES = 67043328
 
 
-def pieces(shape, split_rows, parts):
-    rows = shape[0]
-    if rows % (16 * parts):
-        parts = 1
-    return [(part * (rows // parts), rows // parts) for part in range(parts)]
-
-
-def plan(halves, by_row, small):
+def plan(halves, size):
     chunks = []
-    for at, half in enumerate(halves):
-        parts = max(1, half[0] * half[1] // small)
-        chunks += [(at, start, rows) for start, rows in pieces(half, by_row[at], parts)]
+    for at, (rows, columns) in enumerate(halves):
+        parts = max(1, rows * columns // size)
+        if rows % (16 * parts):
+            parts = 1
+        chunks += [(at, part * (rows // parts), rows // parts) for part in range(parts)]
     return chunks
 
 
-def exchange(n, by_row, chunks, rate, *refs):
+def block(rows, columns, size):
+    step = rows
+    while step % 32 == 0 and step * columns > size:
+        step //= 2
+    return step
+
+
+def coded(slope):
+    scaled = slope * 256.0
+    square = scaled * scaled
+    fourth = square * square
+    eighth = fourth * fourth
+    size = jnp.maximum(eighth, eighth * eighth)
+    return jnp.where(slope < 0.0, -size, size).astype(jnp.bfloat16)
+
+
+def decoded(code):
+    code = code.astype(jnp.float32)
+    power = jnp.log(jnp.abs(code))
+    size = jnp.exp2(jnp.minimum(power * (LOG2E / 8), power * (LOG2E / 16)) - 8.0)
+    return jnp.where(code < 0.0, -size, size)
+
+
+def exchange(n, by_row, chunks, size, rate, *refs):
     m = len(by_row)
     slopes, slope_norm = refs[:m], refs[m]
     params, param_norm = refs[m + 1 : 2 * m + 1], refs[2 * m + 1]
@@ -35,9 +54,9 @@
     halfs, norm_half = refs[:m], refs[m]
     kept, norm_next = refs[m + 1 : 2 * m + 1], refs[2 * m + 1]
     refs = refs[2 * m + 2 :]
-    own, got = refs[:m], refs[m : 2 * m]
-    (norms, norm_own, norm_got, norm_all, in_sem, keep_sem, send_sem, recv_sem,
-     back_send, back_recv, norm_in, norm_send, norm_recv) = refs[2 * m :]
+    own, away, code, got = refs[:m], refs[m : 2 * m], refs[2 * m : 3 * m], refs[3 * m : 4 * m]
+    (norms, norm_own, norm_got, norm_all, away_sem, own_sem, keep_sem, send_sem, recv_sem,
+     back_send, back_recv, norm_in, norm_send, norm_recv) = refs[4 * m :]
 
     me = lax.axis_index("replica")
     peer = 1 - me
@@ -59,59 +78,65 @@
             device_id_type=pl.DeviceIdType.MESH,
         )
 
-    loads = []
+    fetches, loads, sends = [], [], []
     for c, (at, start, rows) in enumerate(chunks):
         mine = pl.ds(start, rows)
+        fetches.append(pltpu.make_async_copy(
+            slopes[at].at[(0, *half_of(at, peer, start, rows))], away[at].at[mine], away_sem.at[c]
+        ))
         loads.append((
             pltpu.make_async_copy(
-                slopes[at].at[(0, *half_of(at, me, start, rows))], own[at].at[mine], in_sem.at[c]
+                slopes[at].at[(0, *half_of(at, me, start, rows))], own[at].at[mine], own_sem.at[c]
             ),
             pltpu.make_async_copy(params[at].at[mine], kept[at].at[mine], keep_sem.at[c]),
         ))
+        sends.append(remote(code[at].at[mine], got[at].at[mine], send_sem.at[c], recv_sem.at[c]))
     norm_loads = (
         pltpu.make_async_copy(slope_norm, norms.at[pl.ds(me, 1)], norm_in.at[0]),
         pltpu.make_async_copy(param_norm, norm_own, norm_in.at[1]),
     )
-
-    barrier = pltpu.get_barrier_semaphore()
-    pl.semaphore_signal(barrier, inc=1, device_id=there, device_id_type=pl.DeviceIdType.MESH)
-    pl.semaphore_wait(barrier, 1)
-
     norm_sends = [
         remote(slope_norm, norms.at[pl.ds(me, 1)], norm_send.at[0], norm_recv.at[0]),
         remote(param_norm, norm_got, norm_send.at[1], norm_recv.at[1]),
     ]
-    sends = [
-        remote(
-            slopes[at].at[(0, *half_of(at, peer, start, rows))],
-            got[at].at[pl.ds(start, rows)],
-            send_sem.at[c],
-            recv_sem.at[c],
-        )
-        for c, (at, start, rows) in enumerate(chunks)
-    ]
-    for send in sends + norm_sends:
-        send.start()
+
+    for fetch in fetches:
+        fetch.start()
+    barrier = pltpu.get_barrier_semaphore()
+    pl.semaphore_signal(barrier, inc=1, device_id=there, device_id_type=pl.DeviceIdType.MESH)
     for load in loads:
         load[0].start()
         load[1].start()
     for load in norm_loads:
         load.start()
+    pl.semaphore_wait(barrier, 1)
+    for send in norm_sends:
+        send.start()
+
+    for c, (at, start, rows) in enumerate(chunks):
+        fetches[c].wait()
+        step = block(rows, kept[at].shape[1], size)
+
+        @pl.loop(0, rows // step)
+        def encode(turn, at=at, start=start, step=step):
+            span = pl.ds(pl.multiple_of(start + turn * step, 16), step)
+            code[at][span] = coded(away[at][span])
+
+        sends[c].start()
 
     backs = []
     for c, (at, start, rows) in enumerate(chunks):
         loads[c][0].wait()
         loads[c][1].wait()
         sends[c].wait_recv()
-        step = 32 if rows % 32 == 0 else 16
-        height, width = kept[at].shape
+        step = block(rows, kept[at].shape[1], size)
 
         @pl.loop(0, rows // step)
-        def update(block, at=at, start=start, step=step, height=height, width=width):
-            first = pl.multiple_of(start + block * step, step)
+        def update(turn, at=at, start=start, step=step):
+            first = pl.multiple_of(start + turn * step, 16)
             span = pl.ds(first, step)
-            mean = (own[at][span] + got[at][span]) * rate
-            moved = kept[at][span] - learn_rate * mean
+            total = own[at][span] + decoded(got[at][span])
+            moved = kept[at][span] - (learn_rate * rate) * total
             kept[at][span] = moved
             halfs[at][half_of(at, me, first, step)] = moved.astype(jnp.bfloat16)
 
@@ -166,14 +191,14 @@
     halves = [param.shape for param in params]
     wholes = [slope.shape[1:] for slope in slopes]
     small = min(half[0] * half[1] for half in halves)
-    chunks = plan(halves, by_row, 4 * small)
+    chunks = plan(halves, small)
     count = len(chunks)
     width = param_norm.shape[0]
     dma = pltpu.SemaphoreType.DMA
     results = sum(rows * columns for rows, columns in wholes) * 2
     results += sum(rows * columns for rows, columns in halves) * 4
     outs = pl.pallas_call(
-        functools.partial(exchange, n, by_row, chunks, n ** (-0.5)),
+        functools.partial(exchange, n, by_row, chunks, small // 2, n ** (-0.5)),
         out_shape=(
             *[pltpu.VMEM(whole, bf16) for whole in wholes],
             pltpu.VMEM((n * width,), bf16),
@@ -184,11 +209,12 @@
         out_specs=[pl.BlockSpec(memory_space=pltpu.VMEM)] * (2 * m + 2),
         scratch_shapes=[
             *[pltpu.VMEM(half, f32) for half in halves * 2],
+            *[pltpu.VMEM(half, bf16) for half in halves * 2],
             pltpu.VMEM((n, n * width), f32),
             pltpu.VMEM((width,), f32),
             pltpu.VMEM((width,), f32),
             pltpu.VMEM((1, n * width), f32),
-            *[dma((count,))] * 6,
+            *[dma((count,))] * 7,
             *[dma((2,))] * 3,
         ],
         compiler_params=pltpu.CompilerParams(

time: 13.6 us -> 12.2 us (0.90)
  Pallas kernels: 12.7 us -> 11.3 us
    pallas_call x1, Pallas kernels: 9.7 us -> 8.3 us  [shards(): pl.pallas_call(functools.partial(exchange, n, by_row, chunks, small // 2,...]
where the time goes in v1:
time: 12.2 us; the launch traced here: 12 us
  Pallas kernels  11.3 us (93%)
  between operations  0.66 us (5%)
    pallas_call x1, Pallas kernels, shards(): pl.pallas_call(functools.partial(exchange, n, by_row, chunks, small // 2,...  8.3 us
    pallas_call x1, Pallas kernels, shards(): pl.pallas_call(functools.partial(settle, len(outs)), out_shape=[jax.Shape...  3.03 us

profile of v1, /device:TPU:3, one launch (start us, length us, event | category | flops | bytes accessed | tf_op | source)
XLA Modules:
  0.0 12.0 jit_solution(7001227017648437116)
XLA Ops:
  0.7 8.3 %exchange.1 = (bf16[768,768]{1,0:T(8,128)(2,1)S(1)}, bf16[768,768]{1,0:T(8,128)(2,1)S(1)}, bf16[192,768]{1,0:T(8,128)(2,1)S(1)}, bf16[192,768]{1,0:T(8,128)(2,1)...) custom-call(f32[1,768,768]{2,1,0:T(8,128)} %refs_0_.1, ...), custom_call_target="tpu_custom_call" | custom-call | tf_op jit(solution)/shard_map/exchange/pallas_call | solution.py:200
  9.0 3.0 %settle.1 = (bf16[768,768]{1,0:T(8,128)(2,1)}, bf16[768,768]{1,0:T(8,128)(2,1)}, bf16[192,768]{1,0:T(8,128)(2,1)}, bf16[192,768]{1,0:T(8,128)(2,1)}, bf16[192,76...) custom-call(bf16[768,768]{1,0:T(8,128)(2,1)S(1)} %get-tuple-element., ...), custom_call_target="tpu_custom_call" | custom-call | tf_op jit(solution)/shard_map/settle/pallas_call | solution.py:225

commit v2 on v1

--- a/solution.py
+++ b/solution.py
@@ -11,11 +11,13 @@
 LOG2E = 1.4426950408889634
 ANY = pl.BlockSpec(memory_space=pl.ANY)
 VMEM_BYTES = 67043328
-
-
-def plan(halves, size):
+ROOM = 1280 * 1024
+
+
+def plan(halves, order, size):
     chunks = []
-    for at, (rows, columns) in enumerate(halves):
+    for at in order:
+        rows, columns = halves[at]
         parts = max(1, rows * columns // size)
         if rows % (16 * parts):
             parts = 1
@@ -46,17 +48,18 @@
     return jnp.where(code < 0.0, -size, size)
 
 
-def exchange(n, by_row, chunks, size, rate, *refs):
+def exchange(n, by_row, spots, chunks, size, rate, *refs):
     m = len(by_row)
     slopes, slope_norm = refs[:m], refs[m]
     params, param_norm = refs[m + 1 : 2 * m + 1], refs[2 * m + 1]
     refs = refs[2 * m + 2 :]
-    halfs, norm_half = refs[:m], refs[m]
-    kept, norm_next = refs[m + 1 : 2 * m + 1], refs[2 * m + 1]
-    refs = refs[2 * m + 2 :]
+    direct = [at for at in range(m) if at not in spots]
+    packed, halfs, norm_half = refs[0], dict(zip(direct, refs[1:])), refs[len(direct) + 1]
+    refs = refs[len(direct) + 2 :]
+    kept, norm_next = refs[:m], refs[m]
+    refs = refs[m + 1 :]
     own, away, code, got = refs[:m], refs[m : 2 * m], refs[2 * m : 3 * m], refs[3 * m : 4 * m]
-    (norms, norm_own, norm_got, norm_all, away_sem, own_sem, keep_sem, send_sem, recv_sem,
-     back_send, back_recv, norm_in, norm_send, norm_recv) = refs[4 * m :]
+    norms, norm_own, norm_got, norm_all, away_sem, recv_sem, own_sem, all_sem, norm_sem = refs[4 * m :]
 
     me = lax.axis_index("replica")
     peer = 1 - me
@@ -78,33 +81,40 @@
             device_id_type=pl.DeviceIdType.MESH,
         )
 
-    fetches, loads, sends = [], [], []
+    def drain(sem, size):
+        part = slopes[0].at[0, pl.ds(0, size // (4 * slopes[0].shape[2]))]
+        pltpu.make_async_copy(part, part, sem).wait()
+
+    fetches, loads, sends = [], {}, []
     for c, (at, start, rows) in enumerate(chunks):
         mine = pl.ds(start, rows)
         fetches.append(pltpu.make_async_copy(
             slopes[at].at[(0, *half_of(at, peer, start, rows))], away[at].at[mine], away_sem.at[c]
         ))
-        loads.append((
+        sends.append(remote(code[at].at[mine], got[at].at[mine], all_sem.at[0], recv_sem.at[c]))
+    for at in dict.fromkeys(at for at, _, _ in chunks):
+        height = kept[at].shape[0]
+        loads[at] = (
             pltpu.make_async_copy(
-                slopes[at].at[(0, *half_of(at, me, start, rows))], own[at].at[mine], own_sem.at[c]
+                slopes[at].at[(0, *half_of(at, me, 0, height))], own[at], own_sem.at[at]
             ),
-            pltpu.make_async_copy(params[at].at[mine], kept[at].at[mine], keep_sem.at[c]),
-        ))
-        sends.append(remote(code[at].at[mine], got[at].at[mine], send_sem.at[c], recv_sem.at[c]))
+            pltpu.make_async_copy(params[at], kept[at], own_sem.at[at]),
+        )
     norm_loads = (
-        pltpu.make_async_copy(slope_norm, norms.at[pl.ds(me, 1)], norm_in.at[0]),
-        pltpu.make_async_copy(param_norm, norm_own, norm_in.at[1]),
+        pltpu.make_async_copy(slope_norm, norms.at[pl.ds(me, 1)], norm_sem.at[0]),
+        pltpu.make_async_copy(param_norm, norm_own, norm_sem.at[1]),
     )
     norm_sends = [
-        remote(slope_norm, norms.at[pl.ds(me, 1)], norm_send.at[0], norm_recv.at[0]),
-        remote(param_norm, norm_got, norm_send.at[1], norm_recv.at[1]),
+        remote(slope_norm, norms.at[pl.ds(me, 1)], norm_sem.at[2], norm_sem.at[3]),
+        remote(param_norm, norm_got, norm_sem.at[4], norm_sem.at[5]),
     ]
 
+    count = len(chunks)
     for fetch in fetches:
         fetch.start()
     barrier = pltpu.get_barrier_semaphore()
     pl.semaphore_signal(barrier, inc=1, device_id=there, device_id_type=pl.DeviceIdType.MESH)
-    for load in loads:
+    for load in loads.values():
         load[0].start()
         load[1].start()
     for load in norm_loads:
@@ -113,37 +123,51 @@
     for send in norm_sends:
         send.start()
 
-    for c, (at, start, rows) in enumerate(chunks):
+    def encode(c):
+        at, start, rows = chunks[c]
         fetches[c].wait()
         step = block(rows, kept[at].shape[1], size)
 
         @pl.loop(0, rows // step)
-        def encode(turn, at=at, start=start, step=step):
+        def turns(turn):
             span = pl.ds(pl.multiple_of(start + turn * step, 16), step)
             code[at][span] = coded(away[at][span])
 
         sends[c].start()
 
-    backs = []
-    for c, (at, start, rows) in enumerate(chunks):
-        loads[c][0].wait()
-        loads[c][1].wait()
+    def update(c):
+        at, start, rows = chunks[c]
+        if start == 0:
+            drain(own_sem.at[at], 8 * kept[at].shape[0] * kept[at].shape[1])
         sends[c].wait_recv()
-        step = block(rows, kept[at].shape[1], size)
+        width = kept[at].shape[1]
+        step = block(rows, width, size)
+        top, fold, columns = spots.get(at, (0, rows, 0))
 
         @pl.loop(0, rows // step)
-        def update(turn, at=at, start=start, step=step):
+        def turns(turn):
             first = pl.multiple_of(start + turn * step, 16)
             span = pl.ds(first, step)
             total = own[at][span] + decoded(got[at][span])
             moved = kept[at][span] - (learn_rate * rate) * total
             kept[at][span] = moved
-            halfs[at][half_of(at, me, first, step)] = moved.astype(jnp.bfloat16)
-
+            if at in spots:
+                row = pl.multiple_of(top + lax.rem(first, fold), 16)
+                column = pl.multiple_of(lax.div(first, fold) * columns, 128)
+                packed[pl.ds(row, step), pl.ds(column, width)] = moved.astype(jnp.bfloat16)
+            else:
+                halfs[at][half_of(at, me, first, step)] = moved.astype(jnp.bfloat16)
+
+        if at in spots:
+            return
         place = half_of(at, me, start, rows)
-        back = remote(halfs[at].at[place], halfs[at].at[place], back_send.at[c], back_recv.at[c])
+        back = remote(halfs[at].at[place], halfs[at].at[place], all_sem.at[1], all_sem.at[2])
         back.start()
-        backs.append(back)
+
+    for c in range(len(chunks)):
+        encode(c)
+    for c in range(len(chunks)):
+        update(c)
 
     for load in norm_loads:
         load.wait()
@@ -160,21 +184,70 @@
     cut = pl.ds(pl.multiple_of(me * width, width), width)
     norm_next[...] = norm_all[0:1, cut].reshape(width)
 
-    for send in sends + norm_sends:
+    for send in norm_sends:
         send.wait_send()
-    for back in backs:
-        back.wait()
-
-
-def settle(count, *refs):
-    sems = refs[-1]
+    sizes = [2 * half.shape[0] * half.shape[1] for half in kept]
+    drain(all_sem.at[0], sum(sizes))
+    back = sum(sizes[at] for at in range(m) if at not in spots)
+    drain(all_sem.at[1], back)
+    drain(all_sem.at[2], back)
+
+
+def half_at(by_row, who, shape, start, rows):
+    height, width = shape
+    if by_row:
+        return pl.ds(pl.multiple_of(who * height + start, 16), rows), pl.ds(0, width)
+    return pl.ds(start, rows), pl.ds(pl.multiple_of(who * width, width), width)
+
+
+def pack(halves, later):
+    width = max(halves[at][1] for at in later)
+    spots, top = {}, 0
+    for at in later:
+        rows, columns = halves[at]
+        spots[at] = (top, rows * columns // width, columns)
+        top += spots[at][1]
+    return spots, (top, width)
+
+
+def unpacked(packed, target, by_row, who, shape, place):
+    top, rows, columns = place
+    return [
+        (
+            packed.at[pl.ds(top, rows), pl.ds(start // rows * columns, columns)],
+            target.at[half_at(by_row, who, shape, start, rows)],
+        )
+        for start in range(0, shape[0], rows)
+    ]
+
+
+def settle(by_row, shapes, spots, *refs):
+    m = len(by_row)
+    count = 2 * m + 2
+    packed, ready, outs, sems = refs[0], refs[1 : -1 - count], refs[-1 - count : -1], refs[-1]
+    me = lax.axis_index("replica")
+    plain = [out for k, out in enumerate(outs) if k not in spots]
     copies = [
-        pltpu.make_async_copy(refs[k], refs[count + k], sems.at[k]) for k in range(count)
+        pltpu.make_async_copy(source, target, sems.at[1 + k])
+        for k, (source, target) in enumerate(zip(ready, plain))
     ]
+    for at in spots:
+        for pair in unpacked(packed, outs[at], by_row[at], me, shapes[at], spots[at]):
+            pltpu.make_async_copy(*pair, sems.at[0]).start()
     for copy in copies:
         copy.start()
     for copy in copies:
         copy.wait()
+    pltpu.make_async_copy(packed, packed, sems.at[0]).wait()
+
+
+def finish(by_row, shapes, spots, *refs):
+    packed, outs, sem = refs[0], refs[-1 - len(spots) : -1], refs[-1]
+    peer = 1 - lax.axis_index("replica")
+    for out, at in zip(outs, spots):
+        for pair in unpacked(packed, out, by_row[at], peer, shapes[at], spots[at]):
+            pltpu.make_async_copy(*pair, sem).start()
+    pltpu.make_async_copy(packed, packed, sem).wait()
 
 
 def shards(n, *arrays):
@@ -191,22 +264,27 @@
     halves = [param.shape for param in params]
     wholes = [slope.shape[1:] for slope in slopes]
     small = min(half[0] * half[1] for half in halves)
-    chunks = plan(halves, small)
+    later = [0,1,5]
+    order = [2, 3, 4, 5, 0, 1]
+    spots, packed = pack(halves, later)
+    chunks = plan(halves, order, 2*small)
     count = len(chunks)
     width = param_norm.shape[0]
     dma = pltpu.SemaphoreType.DMA
-    results = sum(rows * columns for rows, columns in wholes) * 2
+    direct = [wholes[at] for at in range(m) if at not in spots]
+    results = sum(rows * columns for rows, columns in direct + [packed]) * 2
     results += sum(rows * columns for rows, columns in halves) * 4
-    outs = pl.pallas_call(
-        functools.partial(exchange, n, by_row, chunks, small // 2, n ** (-0.5)),
+    kept = pl.pallas_call(
+        functools.partial(exchange, n, by_row, spots, chunks, small // 2, n ** (-0.5)),
         out_shape=(
-            *[pltpu.VMEM(whole, bf16) for whole in wholes],
+            pltpu.VMEM(packed, bf16),
+            *[pltpu.VMEM(whole, bf16) for whole in direct],
             pltpu.VMEM((n * width,), bf16),
             *[pltpu.VMEM(half, f32) for half in halves],
             pltpu.VMEM((width,), f32),
         ),
         in_specs=[ANY] * (2 * m + 2),
-        out_specs=[pl.BlockSpec(memory_space=pltpu.VMEM)] * (2 * m + 2),
+        out_specs=[pl.BlockSpec(memory_space=pltpu.VMEM)] * (len(direct) + m + 3),
         scratch_shapes=[
             *[pltpu.VMEM(half, f32) for half in halves * 2],
             *[pltpu.VMEM(half, bf16) for half in halves * 2],
@@ -214,23 +292,43 @@
             pltpu.VMEM((width,), f32),
             pltpu.VMEM((width,), f32),
             pltpu.VMEM((1, n * width), f32),
-            *[dma((count,))] * 7,
-            *[dma((2,))] * 3,
+            *[dma((count,))] * 2,
+            dma((m,)),
+            dma((3,)),
+            dma((6,)),
         ],
         compiler_params=pltpu.CompilerParams(
-            collective_id=0, has_side_effects=True, vmem_limit_bytes=VMEM_BYTES - results - 192 * 1024
+            collective_id=0, has_side_effects=True, vmem_limit_bytes=VMEM_BYTES - results - ROOM
         ),
         name="exchange",
     )(*slopes, slope_norm, *params, param_norm)
+    swap = [(who, n - 1 - who) for who in range(n)]
+    theirs = lax.ppermute(kept[0], "replica", swap)
+    shapes = wholes + [(n * width,)] + halves + [(width,)]
+    types = [bf16] * (m + 1) + [f32] * (m + 1)
+    small_grant = pltpu.CompilerParams(vmem_limit_bytes=2 * 1024 * 1024)
     outs = list(pl.pallas_call(
-        functools.partial(settle, len(outs)),
-        out_shape=[jax.ShapeDtypeStruct(out.shape, out.dtype) for out in outs],
-        in_specs=[pl.BlockSpec(memory_space=pltpu.VMEM)] * len(outs),
-        out_specs=[ANY] * len(outs),
-        scratch_shapes=[dma((len(outs),))],
-        compiler_params=pltpu.CompilerParams(vmem_limit_bytes=2 * 1024 * 1024),
+        functools.partial(settle, by_row, halves, spots),
+        out_shape=[jax.ShapeDtypeStruct(*out) for out in zip(shapes, types)],
+        in_specs=[pl.BlockSpec(memory_space=pltpu.VMEM)] * len(kept),
+        out_specs=[ANY] * len(shapes),
+        scratch_shapes=[dma((len(kept),))],
+        compiler_params=small_grant,
+        cost_estimate=pl.CostEstimate(flops=10**8, bytes_accessed=results, transcendentals=0),
         name="settle",
-    )(*outs))
+    )(*kept))
+    done = pl.pallas_call(
+        functools.partial(finish, by_row, halves, spots),
+        out_shape=[jax.ShapeDtypeStruct(outs[at].shape, outs[at].dtype) for at in spots],
+        in_specs=[pl.BlockSpec(memory_space=pltpu.VMEM)] + [ANY] * len(spots),
+        out_specs=[ANY] * len(spots),
+        scratch_shapes=[dma(())],
+        input_output_aliases={1 + k: k for k in range(len(spots))},
+        compiler_params=small_grant,
+        name="finish",
+    )(theirs, *[outs[at] for at in spots])
+    for at, whole in zip(spots, done):
+        outs[at] = whole
     for at in turned:
         outs[at] = outs[at].T
         outs[m + 1 + at] = outs[m + 1 + at].T

time: 12.2 us -> 10.9 us (0.89)
  Pallas kernels: 11.3 us -> 9.52 us
  waiting for transfers between devices: 0 us -> 0.32 us
  starting transfers between devices: 0 us -> 0.2 us
    pallas_call x2 -> x3, Pallas kernels: 11.3 us -> 9.52 us  [the longest x1 5.88 us: shards(): pl.pallas_call(functools.partial(exchange, n, by_row, spots, chunks, smal...]
    ppermute x0 -> x1, waiting for transfers between devices: none -> 0.32 us  [shards(): theirs = lax.ppermute(kept[0], 'replica', swap)]
    ppermute x0 -> x1, starting transfers between devices: none -> 0.2 us  [shards(): theirs = lax.ppermute(kept[0], 'replica', swap)]
  transfers between devices with their start and end apart: 0 -> 1, of which waited for: 0 -> 1; matrix products, arithmetic and copies ran while one was open for 0% -> 0% of each run, Pallas kernels for 0% -> 24%
where the time goes in v2:
time: 10.9 us; the launch traced here: 10.7 us
  Pallas kernels  9.52 us (87%)
  between operations  0.67 us (6%)
  waiting for transfers between devices  0.32 us (3%)
  starting transfers between devices  0.2 us (2%)
    pallas_call x1, Pallas kernels, shards(): pl.pallas_call(functools.partial(exchange, n, by_row, spots, chunks, smal...  5.88 us
    pallas_call x1, Pallas kernels, shards(): pl.pallas_call(functools.partial(settle, by_row, halves, spots), out_shap...  2.59 us
    pallas_call x1, Pallas kernels, shards(): pl.pallas_call(functools.partial(finish, by_row, halves, spots), out_shap...  1.05 us
    ppermute x1, waiting for transfers between devices, shards(): theirs = lax.ppermute(kept[0], 'replica', swap)  0.32 us
  transfers between devices with their start and end apart: 1, of which 1 were waited for; matrix products, arithmetic and copies ran while one was open for 0% of the time, Pallas kernels for 24%

profile of v2, /device:TPU:3, one launch (start us, length us, event | category | flops | bytes accessed | tf_op | source)
XLA Modules:
  0.0 10.7 jit_solution(15545111700856295491)
XLA Ops:
  0.7 5.9 %exchange.1 = (bf16[864,768]{1,0:T(8,128)(2,1)S(1)}, bf16[192,768]{1,0:T(8,128)(2,1)S(1)}, bf16[192,768]{1,0:T(8,128)(2,1)S(1)}, bf16[192,768]{1,0:T(8,128)(2,1)...) custom-call(f32[1,768,768]{2,1,0:T(8,128)} %refs_0_.1, ...), custom_call_target="tpu_custom_call" | custom-call | tf_op jit(solution)/shard_map/exchange/pallas_call | solution.py:277
  6.5 0.2 %collective-permute-start = (bf16[864,768]{1,0:T(8,128)(2,1)S(1)}, bf16[864,768]{1,0:T(8,128)(2,1)S(1)}, u32[]{:S(2)}, u32[]{:S(2)}) collective-permute-start(bf16[864,768]{1,0:T(8,128)(2,1)S(1)} %get-tuple-element.43.refs_0_), channel_id=1, source_target_pairs={{0,4},{4,0},{1,5},{5,1},{2,6},{6,2},{3,7},{7,3},{8,12},{12,8},{9,1... | collective-permute-start | bytes 3981320 | tf_op jit(solution)/shard_map/ppermute | solution.py:306
  6.7 2.6 %settle.1 = (bf16[768,768]{1,0:T(8,128)(2,1)}, bf16[768,768]{1,0:T(8,128)(2,1)}, bf16[192,768]{1,0:T(8,128)(2,1)}, bf16[192,768]{1,0:T(8,128)(2,1)}, bf16[192,76...) custom-call(bf16[864,768]{1,0:T(8,128)(2,1)S(1)} %get-tuple-element., ...), custom_call_target="tpu_custom_call" | custom-call | flops 100000000 | bytes 5750784 | tf_op jit(solution)/shard_map/settle/pallas_call | solution.py:310
  9.3 0.3 %collective-permute-done.refs_0_ = bf16[864,768]{1,0:T(8,128)(2,1)S(1)} collective-permute-done((bf16[864,768]{1,0:T(8,128)(2,1)S(1)}, bf16[864,768]{1,0:T(8,128)(2,1)S(1)}, u32[]{:S(2)}, u32[]{:S(2)}) %collective-permute-start) | collective-permute-done | bytes 1327136 | tf_op jit(solution)/shard_map/ppermute | solution.py:306
  9.7 1.1 %finish.1 = (bf16[768,768]{1,0:T(8,128)(2,1)}, bf16[768,768]{1,0:T(8,128)(2,1)}, bf16[192,768]{1,0:T(8,128)(2,1)}) custom-call(bf16[864,768]{1,0:T(8,128)(2,1)S(1)} %collective-permute-done.refs_0_, bf16[768,768]{1,0:T(8,128)(2,1)} %get-tuple-element.55.refs_1_, ...), custom_call_target="tpu_custom_call", output_to_operand_aliasing={{0}: (1, {}), {1}: (2, {}), {2}: (3, {})} | custom-call | tf_op jit(solution)/shard_map/finish/pallas_call | solution.py:320
Async XLA Ops:
  6.5 3.1 %collective-permute-start = (bf16[864,768]{1,0:T(8,128)(2,1)S(1)}, bf16[864,768]{1,0:T(8,128)(2,1)S(1)}, u32[]{:S(2)}, u32[]{:S(2)}) collective-permute-start(bf16[864,768]{1,0:T(8,128)(2,1)S(1)} %get-tuple-element.43.refs_0_), channel_id=1, source_target_pairs={{0,4},{4,0},{1,5},{5,1},{2,6},{6,2},{3,7},{7,3},{8,12},{12,8},{9,1... | collective-permute-start | bytes 3981320 | tf_op jit(solution)/shard_map/ppermute | solution.py:306

commit v3 on v2

--- a/solution.py
+++ b/solution.py
@@ -18,7 +18,7 @@
     chunks = []
     for at in order:
         rows, columns = halves[at]
-        parts = max(1, rows * columns // size)
+        parts = 2 if at == order[0] else max(1, rows * columns // size)
         if rows % (16 * parts):
             parts = 1
         chunks += [(at, part * (rows // parts), rows // parts) for part in range(parts)]
@@ -85,6 +85,10 @@
         part = slopes[0].at[0, pl.ds(0, size // (4 * slopes[0].shape[2]))]
         pltpu.make_async_copy(part, part, sem).wait()
 
+    sizes = [half.shape[0] * half.shape[1] for half in kept]
+    least = min(sizes)
+    big = [at for at in range(m) if sizes[at] > least]
+    group = [1 + big.index(at) if at in big else 0 for at in range(m)]
     fetches, loads, sends = [], {}, []
     for c, (at, start, rows) in enumerate(chunks):
         mine = pl.ds(start, rows)
@@ -96,9 +100,9 @@
         height = kept[at].shape[0]
         loads[at] = (
             pltpu.make_async_copy(
-                slopes[at].at[(0, *half_of(at, me, 0, height))], own[at], own_sem.at[at]
+                slopes[at].at[(0, *half_of(at, me, 0, height))], own[at], own_sem.at[group[at]]
             ),
-            pltpu.make_async_copy(params[at], kept[at], own_sem.at[at]),
+            pltpu.make_async_copy(params[at], kept[at], own_sem.at[group[at]]),
         )
     norm_loads = (
         pltpu.make_async_copy(slope_norm, norms.at[pl.ds(me, 1)], norm_sem.at[0]),
@@ -109,7 +113,6 @@
         remote(param_norm, norm_got, norm_sem.at[4], norm_sem.at[5]),
     ]
 
-    count = len(chunks)
     for fetch in fetches:
         fetch.start()
     barrier = pltpu.get_barrier_semaphore()
@@ -137,8 +140,9 @@
 
     def update(c):
         at, start, rows = chunks[c]
-        if start == 0:
-            drain(own_sem.at[at], 8 * kept[at].shape[0] * kept[at].shape[1])
+        if group[at] not in ready:
+            ready.add(group[at])
+            drain(own_sem.at[group[at]], 8 * sum(sizes[k] for k in range(m) if group[k] == group[at]))
         sends[c].wait_recv()
         width = kept[at].shape[1]
         step = block(rows, width, size)
@@ -161,9 +165,10 @@
         if at in spots:
             return
         place = half_of(at, me, start, rows)
-        back = remote(halfs[at].at[place], halfs[at].at[place], all_sem.at[1], all_sem.at[2])
+        back = remote(halfs[at].at[place], halfs[at].at[place], all_sem.at[0], all_sem.at[1])
         back.start()
 
+    ready = set()
     for c in range(len(chunks)):
         encode(c)
     for c in range(len(chunks)):
@@ -186,11 +191,9 @@
 
     for send in norm_sends:
         send.wait_send()
-    sizes = [2 * half.shape[0] * half.shape[1] for half in kept]
-    drain(all_sem.at[0], sum(sizes))
-    back = sum(sizes[at] for at in range(m) if at not in spots)
+    back = 2 * sum(sizes[at] for at in range(m) if at not in spots)
+    drain(all_sem.at[0], 2 * sum(sizes) + back)
     drain(all_sem.at[1], back)
-    drain(all_sem.at[2], back)
 
 
 def half_at(by_row, who, shape, start, rows):
@@ -227,18 +230,22 @@
     packed, ready, outs, sems = refs[0], refs[1 : -1 - count], refs[-1 - count : -1], refs[-1]
     me = lax.axis_index("replica")
     plain = [out for k, out in enumerate(outs) if k not in spots]
-    copies = [
-        pltpu.make_async_copy(source, target, sems.at[1 + k])
-        for k, (source, target) in enumerate(zip(ready, plain))
-    ]
+    pairs = {None: []}
     for at in spots:
-        for pair in unpacked(packed, outs[at], by_row[at], me, shapes[at], spots[at]):
-            pltpu.make_async_copy(*pair, sems.at[0]).start()
-    for copy in copies:
-        copy.start()
-    for copy in copies:
-        copy.wait()
-    pltpu.make_async_copy(packed, packed, sems.at[0]).wait()
+        pairs[None] += unpacked(packed, outs[at], by_row[at], me, shapes[at], spots[at])
+    for pair in zip(ready, plain):
+        shape = pair[0].shape
+        key = (shape, str(pair[0].dtype)) if len(shape) == 2 else shape
+        pairs.setdefault(key, []).append(pair)
+    for k, same in enumerate(pairs.values()):
+        for pair in same:
+            pltpu.make_async_copy(*pair, sems.at[k]).start()
+    for k, same in enumerate(pairs.values()):
+        source, target = same[0]
+        if len(same) > 1:
+            size = sum(source.size * source.dtype.itemsize for source, _ in same)
+            source = target = packed.at[pl.ds(0, size // (2 * packed.shape[1]))]
+        pltpu.make_async_copy(source, target, sems.at[k]).wait()
 
 
 def finish(by_row, shapes, spots, *refs):
@@ -264,7 +271,8 @@
     halves = [param.shape for param in params]
     wholes = [slope.shape[1:] for slope in slopes]
     small = min(half[0] * half[1] for half in halves)
-    later = [0,1,5]
+    later = [0, 1, 5]
+    smalls = sum(half[0] * half[1] == small for half in halves)
     order = [2, 3, 4, 5, 0, 1]
     spots, packed = pack(halves, later)
     chunks = plan(halves, order, 2*small)
@@ -293,8 +301,8 @@
             pltpu.VMEM((width,), f32),
             pltpu.VMEM((1, n * width), f32),
             *[dma((count,))] * 2,
-            dma((m,)),
-            dma((3,)),
+            dma((1 + m - smalls,)),
+            dma((2,)),
             dma((6,)),
         ],
         compiler_params=pltpu.CompilerParams(

time: 10.9 us -> 10.8 us (level)
  no operation moved by 1% of the time
where the time goes in v3:
time: 10.8 us; the launch traced here: 10.6 us
  Pallas kernels  9.44 us (87%)
  between operations  0.67 us (6%)
  waiting for transfers between devices  0.32 us (3%)
  starting transfers between devices  0.2 us (2%)
    pallas_call x1, Pallas kernels, shards(): pl.pallas_call(functools.partial(exchange, n, by_row, spots, chunks, smal...  5.8 us
    pallas_call x1, Pallas kernels, shards(): pl.pallas_call(functools.partial(settle, by_row, halves, spots), out_shap...  2.59 us
    pallas_call x1, Pallas kernels, shards(): pl.pallas_call(functools.partial(finish, by_row, halves, spots), out_shap...  1.05 us
    ppermute x1, waiting for transfers between devices, shards(): theirs = lax.ppermute(kept[0], 'replica', swap)  0.32 us
  transfers between devices with their start and end apart: 1, of which 1 were waited for; matrix products, arithmetic and copies ran while one was open for 0% of the time, Pallas kernels for 24%

profile of v3, /device:TPU:3, one launch (start us, length us, event | category | flops | bytes accessed | tf_op | source)
XLA Modules:
  0.0 10.6 jit_solution(2378151919876137933)
XLA Ops:
  0.7 5.8 %exchange.1 = (bf16[864,768]{1,0:T(8,128)(2,1)S(1)}, bf16[192,768]{1,0:T(8,128)(2,1)S(1)}, bf16[192,768]{1,0:T(8,128)(2,1)S(1)}, bf16[192,768]{1,0:T(8,128)(2,1)...) custom-call(f32[1,768,768]{2,1,0:T(8,128)} %refs_0_.1, ...), custom_call_target="tpu_custom_call" | custom-call | tf_op jit(solution)/shard_map/exchange/pallas_call | solution.py:285
  6.5 0.2 %collective-permute-start = (bf16[864,768]{1,0:T(8,128)(2,1)S(1)}, bf16[864,768]{1,0:T(8,128)(2,1)S(1)}, u32[]{:S(2)}, u32[]{:S(2)}) collective-permute-start(bf16[864,768]{1,0:T(8,128)(2,1)S(1)} %get-tuple-element.43.refs_0_), channel_id=1, source_target_pairs={{0,4},{4,0},{1,5},{5,1},{2,6},{6,2},{3,7},{7,3},{8,12},{12,8},{9,1... | collective-permute-start | bytes 3981320 | tf_op jit(solution)/shard_map/ppermute | solution.py:314
  6.7 2.6 %settle.1 = (bf16[768,768]{1,0:T(8,128)(2,1)}, bf16[768,768]{1,0:T(8,128)(2,1)}, bf16[192,768]{1,0:T(8,128)(2,1)}, bf16[192,768]{1,0:T(8,128)(2,1)}, bf16[192,76...) custom-call(bf16[864,768]{1,0:T(8,128)(2,1)S(1)} %get-tuple-element., ...), custom_call_target="tpu_custom_call" | custom-call | flops 100000000 | bytes 5750784 | tf_op jit(solution)/shard_map/settle/pallas_call | solution.py:318
  9.3 0.3 %collective-permute-done.refs_0_ = bf16[864,768]{1,0:T(8,128)(2,1)S(1)} collective-permute-done((bf16[864,768]{1,0:T(8,128)(2,1)S(1)}, bf16[864,768]{1,0:T(8,128)(2,1)S(1)}, u32[]{:S(2)}, u32[]{:S(2)}) %collective-permute-start) | collective-permute-done | bytes 1327136 | tf_op jit(solution)/shard_map/ppermute | solution.py:314
  9.6 1.1 %finish.1 = (bf16[768,768]{1,0:T(8,128)(2,1)}, bf16[768,768]{1,0:T(8,128)(2,1)}, bf16[192,768]{1,0:T(8,128)(2,1)}) custom-call(bf16[864,768]{1,0:T(8,128)(2,1)S(1)} %collective-permute-done.refs_0_, bf16[768,768]{1,0:T(8,128)(2,1)} %get-tuple-element.55.refs_1_, ...), custom_call_target="tpu_custom_call", output_to_operand_aliasing={{0}: (1, {}), {1}: (2, {}), {2}: (3, {})} | custom-call | tf_op jit(solution)/shard_map/finish/pallas_call | solution.py:328
Async XLA Ops:
  6.5 3.1 %collective-permute-start = (bf16[864,768]{1,0:T(8,128)(2,1)S(1)}, bf16[864,768]{1,0:T(8,128)(2,1)S(1)}, u32[]{:S(2)}, u32[]{:S(2)}) collective-permute-start(bf16[864,768]{1,0:T(8,128)(2,1)S(1)} %get-tuple-element.43.refs_0_), channel_id=1, source_target_pairs={{0,4},{4,0},{1,5},{5,1},{2,6},{6,2},{3,7},{7,3},{8,12},{12,8},{9,1... | collective-permute-start | bytes 3981320 | tf_op jit(solution)/shard_map/ppermute | solution.py:314
